TPU v7x, 32 devices: a whole 2x2x4 slice. The times are simulated.
32 devices in a mesh: row: 4 (over y, core), col: 8 (over z, x).
Axes of the slice: x: 2, y: 2, z: 4, core: 2. Of those that a mesh axis runs over, the one named last changes fastest.
Arguments:
- constraint: bfloat16 [8192, 16384], P('row', 'col'), may hold values from -0.046875 to 0.046875
- pattern: int32 [64, 128], P('row', 'col'), may hold values 0 or 1
- objective: float32 [16384, 256], P('col'), may hold values from -31 to 31
- row_bound: float32 [8192, 256], P('row'), may hold values from -31 to 31
- lower_bound: float32 [16384], P('col'), may hold values from -2 to -0.5
- upper_bound: float32 [16384], P('col'), may hold values from 0.5 to 2
Outputs:
- primal: float32 [16384, 256], P('col')
- dual_values: float32 [8192, 256], P('row')
- residual_norms: float32 [256], replicated
All inputs are finite; a program needn't handle non-finite values. No bound on the sum of `pattern` on one device may be relied on, other than what follows from the above.
Results may differ from a plain program's by a relative error of at most 0.0019.
Values may be sent and summed in bfloat16 or wider, within the bound.
No kernel may reach another device: no remote copies, remote signals or barrier semaphores. Data moves between devices by JAX's collectives and lax.ppermute only.
A program may use at most 128 MiB of HBM per device.

v0:
```python
import jax
import jax.numpy as jnp
from jax import lax
from jax.sharding import PartitionSpec as P

BLOCK = 128
ITERS = 3
step_primal = 0.6
step_dual = 0.6
epsilon = 1e-06


def masked(constraint, pattern):
    row_blocks, col_blocks = pattern.shape
    blocks = (
        constraint.reshape(row_blocks, BLOCK, col_blocks, BLOCK)
        * pattern.astype(jnp.bfloat16)[:, None, :, None]
    )
    return blocks.reshape(row_blocks * BLOCK, col_blocks * BLOCK)


def transposed(matrix, values):
    return lax.dot_general(
        matrix, values, (((0,), (0,)), ((), ())), preferred_element_type=jnp.float32
    )


def partial_stats(slack_share, displacement):
    return jnp.stack(
        [jnp.sum(jnp.maximum(slack_share, 0.0) ** 2, axis=0), jnp.sum(displacement**2, axis=0)]
    )


def settle(record):
    return lax.psum(record, ("row", "col"))


def on_device(constraint, pattern, objective, row_bound, lower_bound, upper_bound):
    matrix = masked(constraint, pattern)
    local_rows, local_cols = matrix.shape
    batch_size = objective.shape[1]
    row_devices = lax.axis_size("row")
    col_devices = lax.axis_size("col")
    total_rows = local_rows * row_devices
    total_cols = local_cols * col_devices
    row_share = local_rows // col_devices
    col_share = local_cols // row_devices
    row_offset = lax.axis_index("col") * row_share
    col_offset = lax.axis_index("row") * col_share
    records = []
    lower_share = lower_bound[:, None]
    upper_share = upper_bound[:, None]
    primal = jnp.zeros((local_cols, batch_size), jnp.float32)
    dual_values = jnp.zeros((local_rows, batch_size), jnp.float32)
    for iteration in range(ITERS):
        if iteration == 0:
            gradient = objective
        else:
            gradient = objective - lax.psum(
                transposed(matrix, dual_values.astype(jnp.bfloat16)), "row"
            )
        updated = jnp.clip(primal - step_primal * gradient, lower_share, upper_share)
        extrapolated = (2.0 * updated - primal).astype(jnp.bfloat16)
        product_rows = lax.psum(
            jnp.dot(matrix, extrapolated, preferred_element_type=jnp.float32), "col"
        )
        slack_rows = row_bound - product_rows
        dual_values = jnp.maximum(dual_values + step_dual * slack_rows, 0.0)
        slack_share = lax.dynamic_slice_in_dim(slack_rows, row_offset, row_share, 0)
        displacement = lax.dynamic_slice_in_dim(updated - primal, col_offset, col_share, 0)
        records.append(settle(partial_stats(slack_share, displacement)))
        primal = updated
    stacked = jnp.stack(records)
    residual_norms = jnp.zeros((batch_size,), jnp.float32)
    for iteration in range(ITERS):
        residual_norms = (
            residual_norms
            + jnp.sqrt(stacked[iteration, 0] / total_rows + epsilon)
            + jnp.sqrt(stacked[iteration, 1] / total_cols + epsilon)
        )
    return (primal, dual_values, residual_norms)


def solution(mesh):
    placed = (P("row", "col"), P("row", "col"), P("col", None), P("row", None), P("col"), P("col"))
    return jax.shard_map(
        on_device,
        mesh=mesh,
        in_specs=placed,
        out_specs=(P("col", None), P("row", None), P()),
        check_vma=False,
    )
```

profile of v0, /device:TPU:0, one launch (start us, length us, event | category | flops | bytes accessed | tf_op | source)
XLA Modules:
  0.0 529.3 jit_solution(18435655729704046118)
XLA Ops:
  9.1 2.2 copy-done.6
  11.3 1.9 bitcast_multiply_fusion
  13.2 3.2 copy-done.7
  16.4 3.9 fusion.3
  20.4 105.1 %all-reduce.7.cloned.1.call-done = f32[2048,256]{1,0:T(8,128)} async-done(((f32[2048,256]{1,0:T(8,128)}), f32[2048,256]{1,0:T(8,128)}) %all-reduce.7.cloned.1.call-update) | async-done | bytes 2097168 | tf_op jit(solution)/shard_map/psum | solution.py:64
  125.5 1.9 sub.37
  127.4 1.4 copy-done.3
  128.8 7.2 %fusion.1 = f32[2048,256]{1,0:T(8,128)} fusion(bf16[2048,2048]{1,0:T(8,128)(2,1)} %copy-done.7, f32[2048,256]{1,0:T(8,128)S(1)} %sub.37), kind=kOutput, calls=%fused_computation.11 | convolution fusion | flops 2149056512 | bytes 12582912 | tf_op jit(solution)/shard_map/dot_general | solution.py:23
  136.1 50.8 %all-reduce.9.cloned.1.call-done = f32[2048,256]{1,0:T(8,128)} async-done(((f32[2048,256]{1,0:T(8,128)}), f32[2048,256]{1,0:T(8,128)}) %all-reduce.9.cloned.1.call-update) | async-done | bytes 2097168 | tf_op jit(solution)/shard_map/psum | solution.py:59
  186.9 2.7 maximum_minimum_fusion.1
  189.6 1.3 copy-done.1
  190.9 7.3 %fusion.4 = f32[2048,256]{1,0:T(8,128)} fusion(bf16[2048,2048]{1,0:T(8,128)(2,1)} %copy-done.7, f32[2048,256]{1,0:T(8,128)S(1)} %maximum_minimum_fusion.1, f32[2048,256]{1,0:T(8,128)S(1)} %copy-done.9, f32[2048]{0:T(1024)S(1)} %copy-done.11, f32[2048]{0:T(1024)S(1)} %copy-done.12), kind=kOutput, calls=%fused_computation.13 | convolution fusion | flops 2151153664 | bytes 14696448 | tf_op jit(solution)/shard_map/dot_general | solution.py:65
  198.5 102.3 %all-reduce.11.cloned.1.call-done = f32[2048,256]{1,0:T(8,128)} async-done(((f32[2048,256]{1,0:T(8,128)}), f32[2048,256]{1,0:T(8,128)}) %all-reduce.11.cloned.1.call-update) | async-done | bytes 2097168 | tf_op jit(solution)/shard_map/psum | solution.py:64
  300.7 2.0 sub.41
  302.8 1.3 copy-done.5
  304.0 7.3 %fusion.6 = f32[2048,256]{1,0:T(8,128)} fusion(bf16[2048,2048]{1,0:T(8,128)(2,1)} %copy-done.7, f32[2048,256]{1,0:T(8,128)S(1)} %sub.41, f32[2048,256]{1,0:T(8,128)S(1)} %copy-done.4), kind=kOutput, calls=%fused_computation.15 | convolution fusion | flops 2150629376 | bytes 14680064 | tf_op jit(solution)/shard_map/dot_general | solution.py:23
  311.4 50.8 %all-reduce.13.cloned.1.call-done = f32[2048,256]{1,0:T(8,128)} async-done(((f32[2048,256]{1,0:T(8,128)}), f32[2048,256]{1,0:T(8,128)}) %all-reduce.13.cloned.1.call-update) | async-done | bytes 2097168 | tf_op jit(solution)/shard_map/psum | solution.py:59
  362.2 4.4 maximum_minimum_fusion.2
  366.6 1.3 copy-done.10
  367.9 7.1 %fusion.5 = f32[2048,256]{1,0:T(8,128)} fusion(bf16[2048,2048]{1,0:T(8,128)(2,1)} %copy-done.7, f32[2048,256]{1,0:T(8,128)S(1)} %copy-done.2, f32[2048,256]{1,0:T(8,128)S(1)} %get-tuple-element.12), kind=kOutput, calls=%fused_computation.14 | convolution fusion | flops 2149056512 | bytes 14680064 | tf_op jit(solution)/shard_map/dot_general | solution.py:65
  377.0 1.5 multiply_reduce_fusion.1
  378.5 99.0 %all-reduce.15.cloned.1.call-done = f32[2048,256]{1,0:T(8,128)} async-done(((f32[2048,256]{1,0:T(8,128)}), f32[2048,256]{1,0:T(8,128)}) %all-reduce.15.cloned.1.call-update) | async-done | bytes 2097168 | tf_op jit(solution)/shard_map/psum | solution.py:64
  477.5 4.9 add_maximum_fusion
  482.4 39.8 %all-reduce = (f32[1,2,256]{2,1,0:T(2,128)S(1)}, f32[1,2,256]{2,1,0:T(2,128)S(1)}, f32[1,2,256]{2,1,0:T(2,128)S(1)}) all-reduce(f32[1,2,256]{2,1,0:T(2,128)S(1)} %maximum_bitcast_fusion.2, f32[1,2,256]{2,1,0:T(2,128)S(1)} %get-tuple-element.14, f32[1,2,256]{2,1,0:T(2,128)S(1)} %get-tuple-element.13), channel_id=1, replica_groups=mesh['row'=4,'col'=8] {'row','col'}, use_global_device_ids=true, to_apply=%region_13.14 | all-reduce | flops 1536 | bytes 12288 | tf_op jit(solution)/shard_map/psum | solution.py:35
  (38 shorter events, 5.0 us)
Async XLA Ops:
  7.2 118.4 %all-reduce.7.cloned.1.call-start = ((), (), s32[]{:S(2)}) async-start(), calls=%async_computation | async-start | bytes 4194304 | tf_op jit(solution)/shard_map/psum | solution.py:64
  7.9 3.4 copy-start.6
  11.3 5.1 copy-start.8
  11.3 5.1 copy-start.11
  11.3 5.1 copy-start.12
  13.2 3.2 copy-start.7
  20.3 105.2 %copy-start = (f32[2048,256]{1,0:T(8,128)S(1)}, f32[2048,256]{1,0:T(8,128)}, u32[]{:S(2)}) copy-start(f32[2048,256]{1,0:T(8,128)} %param.9) | copy-start | bytes 6291460
  20.3 166.5 %all-reduce.9.cloned.1.call-start = ((), (), s32[]{:S(2)}) async-start(), calls=%async_computation.1 | async-start | bytes 4194304 | tf_op jit(solution)/shard_map/psum | solution.py:59
  127.4 1.4 copy-start.3
  136.0 164.7 %all-reduce.11.cloned.1.call-start = ((), (), s32[]{:S(2)}) async-start(), calls=%async_computation.2 | async-start | bytes 4194304 | tf_op jit(solution)/shard_map/psum | solution.py:64
  186.9 4.0 copy-start.9
  189.6 1.3 copy-start.1
  198.2 163.9 %all-reduce.13.cloned.1.call-start = ((), (), s32[]{:S(2)}) async-start(), calls=%async_computation.3 | async-start | bytes 4194304 | tf_op jit(solution)/shard_map/psum | solution.py:59
  300.7 3.3 copy-start.4
  302.7 1.3 copy-start.5
  311.3 166.1 %all-reduce.15.cloned.1.call-start = ((), (), s32[]{:S(2)}) async-start(), calls=%async_computation.4 | async-start | bytes 4194304 | tf_op jit(solution)/shard_map/psum | solution.py:64
  362.2 5.7 %copy-start.2 = (f32[2048,256]{1,0:T(8,128)S(1)}, f32[2048,256]{1,0:T(8,128)}, u32[]{:S(2)}) copy-start(f32[2048,256]{1,0:T(8,128)} %copy-done.1) | copy-start | bytes 6291460
  366.6 1.3 copy-start.10
Sparse Core Ops, SparseCore 0:
  20.5 105.0 all-reduce.6
  136.2 50.6 all-reduce.8
  198.3 102.3 all-reduce.10
  311.5 50.6 all-reduce.12
  375.1 102.3 all-reduce.14
where the time goes:
time: 530 us; the launch traced here: 529 us
  waiting for transfers between devices  408 us (77%)
  blocking collectives  39.8 us (8%)
  matrix products  32.8 us (6%)
  other arithmetic  22.6 us (4%)
  between operations  13.9 us (3%)
  local copies, waits for them, and re-layouts  11.9 us (2%)
    psum x3, waiting for transfers between devices, on_device(): lax.psum(jnp.dot(matrix, extrapolated, preferred_element_type=jnp.float32...  306 us
    psum x2, waiting for transfers between devices, on_device(): lax.psum(transposed(matrix, dual_values.astype(jnp.bfloat16)), 'row')  102 us
    psum x1, blocking collectives, settle(): return lax.psum(record, ('row', 'col'))  39.8 us
    dot_general x3, matrix products, on_device(): jnp.dot(matrix, extrapolated, preferred_element_type=jnp.float32)  18.3 us
    dot_general x2, matrix products, transposed(): lax.dot_general(matrix, values, (((0,), (0,)), ((), ())), preferred_eleme...  14.5 us
    unnamed x26, local copies, waits for them, and re-layouts  10.8 us
  transfers between devices with their start and end apart: 5, of which 5 were waited for; matrix products, arithmetic and copies ran while one was open for 1% of the time, Pallas kernels for 0%

commit v1 on v0

--- a/solution.py
+++ b/solution.py
@@ -1,13 +1,22 @@
+import functools
 import jax
 import jax.numpy as jnp
 from jax import lax
 from jax.sharding import PartitionSpec as P
+from jax.lax import all_gather
 
 BLOCK = 128
 ITERS = 3
 step_primal = 0.6
 step_dual = 0.6
 epsilon = 1e-06
+
+
+def node_change(in_array, axis_key):
+    return all_gather(in_array, axis_name=axis_key).sum(axis=0)
+
+
+keep_up_trails_on_mesh = functools.partial(node_change, axis_key="col")
 
 
 def masked(constraint, pattern):
@@ -61,8 +70,8 @@
             )
         updated = jnp.clip(primal - step_primal * gradient, lower_share, upper_share)
         extrapolated = (2.0 * updated - primal).astype(jnp.bfloat16)
-        product_rows = lax.psum(
-            jnp.dot(matrix, extrapolated, preferred_element_type=jnp.float32), "col"
+        product_rows = keep_up_trails_on_mesh(
+            jnp.dot(matrix, extrapolated, preferred_element_type=jnp.float32)
         )
         slack_rows = row_bound - product_rows
         dual_values = jnp.maximum(dual_values + step_dual * slack_rows, 0.0)

time: 530 us -> 927 us (1.75)
  waiting for transfers between devices: 408 us -> 781 us
  other arithmetic: 22.6 us -> 48.1 us
    all_gather x0 -> x3, waiting for transfers between devices: none -> 681 us  [node_change(): return all_gather(in_array, axis_name=axis_key).sum(axis=0)]
    psum x3 -> x0, waiting for transfers between devices: 306 us -> none  [on_device(): lax.psum(jnp.dot(matrix, extrapolated, preferred_element_type=jnp.float32...]
    reduce_sum x0 -> x3, other arithmetic: none -> 25.5 us  [node_change(): return all_gather(in_array, axis_name=axis_key).sum(axis=0)]
  transfers between devices with their start and end apart: 5 -> 5, of which waited for: 5 -> 5; matrix products, arithmetic and copies ran while one was open for 1% -> 0% of each run, Pallas kernels for 0% -> 0%
where the time goes in v1:
time: 927 us; the launch traced here: 926 us
  waiting for transfers between devices  781 us (84%)
  other arithmetic  48.1 us (5%)
  blocking collectives  38.5 us (4%)
  matrix products  32.8 us (4%)
  between operations  13.9 us (1%)
  local copies, waits for them, and re-layouts  11.9 us (1%)
    all_gather x3, waiting for transfers between devices, node_change(): return all_gather(in_array, axis_name=axis_key).sum(axis=0)  681 us
    psum x2, waiting for transfers between devices, on_device(): lax.psum(transposed(matrix, dual_values.astype(jnp.bfloat16)), 'row')  99.3 us
    psum x1, blocking collectives, settle(): return lax.psum(record, ('row', 'col'))  38.5 us
    reduce_sum x3, other arithmetic, node_change(): return all_gather(in_array, axis_name=axis_key).sum(axis=0)  25.5 us
  transfers between devices with their start and end apart: 5, of which 5 were waited for; matrix products, arithmetic and copies ran while one was open for 0% of the time, Pallas kernels for 0%

profile of v1, /device:TPU:0, one launch (start us, length us, event | category | flops | bytes accessed | tf_op | source)
XLA Modules:
  0.0 926.3 jit_solution(1521369840371373175)
XLA Ops:
  9.1 2.2 copy-done.6
  11.3 1.9 bitcast_multiply_fusion
  13.2 3.2 copy-done.7
  16.4 3.9 fusion.3
  20.4 230.1 %all-gather.7.cloned.1.call-done = f32[16384,256]{1,0:T(8,128)} async-done(((f32[2048,256]{1,0:T(8,128)}), f32[16384,256]{1,0:T(8,128)}) %all-gather.7.cloned.1.call-update) | async-done | bytes 16777232 | tf_op jit(solution)/shard_map/all_gather | solution.py:16
  250.5 8.6 reduce_sum.81
  259.1 1.9 sub.37
  260.9 1.4 copy-done.3
  262.3 7.2 fusion.1
  269.6 49.7 %all-reduce.4.cloned.1.call-done = f32[2048,256]{1,0:T(8,128)} async-done(((f32[2048,256]{1,0:T(8,128)}), f32[2048,256]{1,0:T(8,128)}) %all-reduce.4.cloned.1.call-update) | async-done | bytes 2097168 | tf_op jit(solution)/shard_map/psum | solution.py:68
  319.3 2.7 maximum_minimum_fusion.1
  323.3 7.3 fusion.4
  330.9 227.3 %all-gather.9.cloned.1.call-done = f32[16384,256]{1,0:T(8,128)} async-done(((f32[2048,256]{1,0:T(8,128)}), f32[16384,256]{1,0:T(8,128)}) %all-gather.9.cloned.1.call-update) | async-done | bytes 16777232 | tf_op jit(solution)/shard_map/all_gather | solution.py:16
  558.2 8.5 reduce_sum.82
  566.6 2.0 sub.41
  569.9 7.3 fusion.6
  577.3 49.7 %all-reduce.6.cloned.1.call-done = f32[2048,256]{1,0:T(8,128)} async-done(((f32[2048,256]{1,0:T(8,128)}), f32[2048,256]{1,0:T(8,128)}) %all-reduce.6.cloned.1.call-update) | async-done | bytes 2097168 | tf_op jit(solution)/shard_map/psum | solution.py:68
  627.0 4.4 maximum_minimum_fusion.2
  632.7 7.1 fusion.5
  641.8 1.5 multiply_reduce_fusion.1
  643.3 224.0 %all-gather.11.cloned.1.call-done = f32[16384,256]{1,0:T(8,128)} async-done(((f32[2048,256]{1,0:T(8,128)}), f32[16384,256]{1,0:T(8,128)}) %all-gather.11.cloned.1.call-update) | async-done | bytes 16777232 | tf_op jit(solution)/shard_map/all_gather | solution.py:16
  867.3 8.5 reduce_sum.83
  875.7 4.9 add_maximum_fusion
  880.7 38.5 %all-reduce = (f32[1,2,256]{2,1,0:T(2,128)S(1)}, f32[1,2,256]{2,1,0:T(2,128)S(1)}, f32[1,2,256]{2,1,0:T(2,128)S(1)}) all-reduce(f32[1,2,256]{2,1,0:T(2,128)S(1)} %maximum_bitcast_fusion.2, f32[1,2,256]{2,1,0:T(2,128)S(1)} %get-tuple-element.14, f32[1,2,256]{2,1,0:T(2,128)S(1)} %get-tuple-element.13), channel_id=1, replica_groups=mesh['row'=4,'col'=8] {'row','col'}, use_global_device_ids=true, to_apply=%region_13.14 | all-reduce | flops 1536 | bytes 12288 | tf_op jit(solution)/shard_map/psum | solution.py:44
  (41 shorter events, 8.9 us)
Async XLA Ops:
  7.2 243.3 %all-gather.7.cloned.1.call-start = ((), (), s32[]{:S(2)}) async-start(), calls=%async_computation.2 | async-start | bytes 18874368 | tf_op jit(solution)/shard_map/all_gather | solution.py:16
  7.9 3.4 copy-start.6
  11.3 5.1 copy-start.8
  11.3 5.1 copy-start.11
  11.3 5.1 copy-start.12
  13.2 3.2 copy-start.7
  20.3 299.0 %all-reduce.4.cloned.1.call-start = ((), (), s32[]{:S(2)}) async-start(), calls=%async_computation | async-start | bytes 4194304 | tf_op jit(solution)/shard_map/psum | solution.py:68
  250.5 8.6 copy-start
  260.9 1.4 copy-start.3
  269.6 288.6 %all-gather.9.cloned.1.call-start = ((), (), s32[]{:S(2)}) async-start(), calls=%async_computation.3 | async-start | bytes 18874368 | tf_op jit(solution)/shard_map/all_gather | solution.py:16
  319.3 4.0 copy-start.9
  322.0 1.3 copy-start.1
  330.7 296.3 %all-reduce.6.cloned.1.call-start = ((), (), s32[]{:S(2)}) async-start(), calls=%async_computation.1 | async-start | bytes 4194304 | tf_op jit(solution)/shard_map/psum | solution.py:68
  566.6 3.3 copy-start.4
  568.6 1.3 copy-start.5
  577.2 290.0 %all-gather.11.cloned.1.call-start = ((), (), s32[]{:S(2)}) async-start(), calls=%async_computation.4 | async-start | bytes 18874368 | tf_op jit(solution)/shard_map/all_gather | solution.py:16
  627.0 5.7 copy-start.2
  631.4 1.3 copy-start.10
Sparse Core Ops, SparseCore 0:
  20.5 229.9 all-gather.6
  269.7 49.5 all-reduce.3
  330.8 227.3 all-gather.8
  577.4 49.5 all-reduce.5
  639.9 227.3 all-gather.10
